TPU v7x, 512 devices: a whole 4x8x8 slice. The times are simulated.
512 devices in a mesh: dp: 16 (over y_lo, x), space: 32 (over z, y_hi, core).
Axes of the slice: x: 4, y: 8 (y_hi: 2, y_lo: 4; y = y_hi * 4 + y_lo), z: 8, core: 2. Of those that a mesh axis runs over, the one named last changes fastest.
Arguments:
- fields: bfloat16 [16, 100, 131072], P('dp', None, 'space'), may hold values from -6 to 6
- cell_index: int32 [1024, 128], P('space'), may hold values from 0 to 6143
- interp_weight: bfloat16 [1024, 16, 128], P('space'), may hold values from 0 to 2, as said below
- w_in: bfloat16 [100, 1024], replicated, may hold values from -0.625 to 0.625
- ln_gain: float32 [1024], replicated, may hold values from 0.5 to 1.5
- w_qkv: bfloat16 [1024, 3072], P('dp'), may hold values from -0.1875 to 0.1875
- w_out: bfloat16 [1024, 1024], P('dp'), may hold values from -3 to 3
Outputs:
- latent: bfloat16 [16, 16384, 1024], P('dp', 'space')
- update: bfloat16 [16, 16384, 1024], P('dp', 'space')
Inputs may be any that keep to these rules, and one draw needn't show every extreme that they name: `interp_weight`: in each block the slots from some count on carry zero weight for all its 16 nodes; that count lies between 48 and 128. `cell_index`: indexes a shard's 4096 cells extended by 1024 cells of each neighbouring shard, lower neighbour first.
All inputs are finite; a program needn't handle non-finite values.
Results may differ from a plain program's by a relative error of at most 0.0068.
Values may be sent and summed in bfloat16 or wider, within the bound.
A program may use at most 128 MiB of HBM per device.

v0:
```python
import functools

import jax
import jax.numpy as jnp
from jax import lax
from jax.experimental import pallas as pl
from jax.experimental.pallas import tpu as pltpu
from jax.sharding import PartitionSpec as P

HEADS = 16
GROUP_HEADS = 4
F32, BF16 = jnp.float32, jnp.bfloat16
MESH = pl.DeviceIdType.MESH


def kernel(
    n, space, index_ref, field_ref, weight_ref, w_in_ref, gain_ref, w_qkv_ref, w_out_ref,
    att_out, w_out_full, enc_out,
    low_ref, high_ref, cells_ref, picked_ref, enc_ref, w_in_full, normed_ref, qkv_ref, out_ref,
    q_ref, k_ref, v_ref, att_ref,
    local_sem, leave_sem, field_send, field_recv, enc_send, enc_recv,
    a_send, a_recv, f_send, f_recv, p_send, p_recv,
):
    d, s = lax.axis_index("dp"), lax.axis_index("space")
    up, down = lax.rem(s + 1, space), lax.rem(s + space - 1, space)
    core = lax.rem(s, 2)
    partner = s + 1 - 2 * core
    channels, cell_count = field_ref.shape
    reach = low_ref.shape[1]
    rows = w_qkv_ref.shape[0]
    half = rows // 2
    quarter = half // 2
    width = w_out_ref.shape[1]
    groups, _, gw3 = qkv_ref.shape
    gw = gw3 // 3
    head_size = gw // GROUP_HEADS
    nodes = att_out.shape[0]
    margin = nodes // 2
    window = nodes + 2 * margin
    blocks, per_block, slots = weight_ref.shape
    if n == 4:
        peers = [d + 1 - 2 * lax.rem(d, 2), lax.rem(d + 2, 4), 3 - d]
    else:
        peers = [lax.rem(d + i, n) for i in range(1, n)]

    local = []
    for g in range(groups):
        for t in range(3):
            local.append(pltpu.make_async_copy(
                w_qkv_ref.at[:, pl.ds(t * width + g * gw, gw)],
                qkv_ref.at[g, pl.ds(pl.multiple_of(d * rows, rows), rows), pl.ds(t * gw, gw)],
                local_sem.at[len(local)]))
    local.append(pltpu.make_async_copy(
        w_out_ref, out_ref.at[pl.ds(pl.multiple_of(d * rows, rows), rows), :],
        local_sem.at[len(local)]))
    for copy in local:
        copy.start()

    barrier = pltpu.get_barrier_semaphore()
    for peer in peers:
        pl.semaphore_signal(barrier, inc=1, device_id=(peer, s), device_id_type=MESH)
    for peer in (up, down):
        pl.semaphore_signal(barrier, inc=1, device_id=(d, peer), device_id_type=MESH)
    pl.semaphore_wait(barrier, len(peers) + 2)

    def remote(src, dst, send, recv, device):
        return pltpu.make_async_remote_copy(
            src_ref=src, dst_ref=dst, send_sem=send, recv_sem=recv,
            device_id=device, device_id_type=MESH)

    field_up = remote(field_ref.at[:, pl.ds(cell_count - reach, reach)], low_ref,
                      field_send.at[0], field_recv.at[0], (d, up))
    field_down = remote(field_ref.at[:, pl.ds(0, reach)], high_ref,
                        field_send.at[1], field_recv.at[1], (d, down))
    field_up.start()
    field_down.start()

    def piece(c, slot, lo, size):
        span = pl.ds(pl.multiple_of(slot * rows + lo, size), size)
        return out_ref.at[span, :] if c == groups else qkv_ref.at[c, span, :]

    def own_copy(c, i):
        ref = piece(c, d, core * half, half)
        return remote(ref, ref, a_send.at[c, i], a_recv.at[c, i], (peers[i], s))

    def own_recv(c, i):
        source = peers[i] if n == 4 else peers[n - 2 - i]
        ref = piece(c, source, core * half, half)
        return remote(ref, ref, a_send.at[c, i], a_recv.at[c, i], (peers[i], s)), source

    def swap(c, i, slot, side):
        ref = piece(c, slot, side * half, half)
        return remote(ref, ref, p_send.at[c, i], p_recv.at[c, i], (d, partner))

    direct = 2 if n == 4 else n - 1

    def begin(c):
        mine = local[3 * c:3 * c + 3] if c < groups else local[-1:]
        for copy in mine:
            copy.wait()
        for i in range(direct):
            own_copy(c, i).start()

    def onward(c, i, slot):
        ref = piece(c, slot, core * half + i * quarter, quarter)
        return remote(ref, ref, f_send.at[c, i], f_recv.at[c, i], (peers[1 - i], s))

    def forward(c):
        for i in range(direct):
            copy, source = own_recv(c, i)
            copy.wait_recv()
            if n == 4:
                onward(c, i, source).start()
            swap(c, i, source, core).start()

    def finish(c):
        if n == 4:
            for i in range(2):
                onward(c, i, peers[2]).wait_recv()
            swap(c, 2, peers[2], core).start()
        for i in range(n - 1):
            source = peers[i] if n == 4 else peers[n - 2 - i]
            swap(c, i, source, 1 - core).wait_recv()

    def drain(c):
        for i in range(direct):
            own_copy(c, i).wait_send()
        if n == 4:
            for i in range(2):
                onward(c, i, peers[i]).wait_send()
        for i in range(n - 1):
            source = peers[i] if n == 4 else peers[n - 2 - i]
            swap(c, i, source, core).wait_send()

    begin(0)
    begin(1)
    begin(2)

    unit = (lax.broadcasted_iota(jnp.int32, (channels, 128), 0)
            == lax.broadcasted_iota(jnp.int32, (channels, 128), 1)).astype(BF16)

    def turn(source, start, target):
        cells_ref[pl.ds(target, 512), :] = lax.dot_general(
            source[:, pl.ds(start, 512)], unit, (((0,), (0,)), ((), ())),
            preferred_element_type=F32)

    @pl.loop(0, cell_count // 512, unroll=2)
    def _(i):
        turn(field_ref, pl.multiple_of(i * 512, 512), pl.multiple_of(reach + i * 512, 512))

    pad = w_in_full.shape[0]
    w_in_full[pl.ds(pad - 32, 32), :] = jnp.zeros((32, width), BF16)
    w_in_full[pl.ds(0, channels), :] = w_in_ref[...]

    field_up.wait_recv()
    field_down.wait_recv()

    @pl.loop(0, reach // 512)
    def _(i):
        turn(low_ref, pl.multiple_of(i * 512, 512), pl.multiple_of(i * 512, 512))
        turn(high_ref, pl.multiple_of(i * 512, 512),
             pl.multiple_of(reach + cell_count + i * 512, 512))

    def gather(first, last):
        @pl.loop(first, last)
        def _(b):
            base = pl.multiple_of(b * slots, slots)
            for j in range(slots):
                picked_ref[pl.ds(base + j, 1), :] = cells_ref[pl.ds(index_ref[b, j], 1), :]

    gather(0, blocks // 2)
    forward(0)
    begin(3)
    gather(blocks // 2, blocks)

    per_step = 8

    @pl.loop(0, blocks // per_step)
    def _(i):
        for j in range(per_step):
            b = i * per_step + j
            rows_b = picked_ref[pl.ds(pl.multiple_of(b * slots, slots), slots), :].astype(BF16)
            enc_ref[pl.ds(pl.multiple_of(margin + b * per_block, per_block), per_block), :] = jnp.dot(
                weight_ref[b], rows_b, preferred_element_type=F32).astype(BF16)

    enc_up = remote(enc_ref.at[pl.ds(nodes, margin), :], enc_ref.at[pl.ds(0, margin), :],
                    enc_send.at[0], enc_recv.at[0], (d, up))
    enc_down = remote(enc_ref.at[pl.ds(margin, margin), :],
                      enc_ref.at[pl.ds(margin + nodes, margin), :],
                      enc_send.at[1], enc_recv.at[1], (d, down))
    enc_up.start()
    enc_down.start()
    enc_leave = pltpu.make_async_copy(enc_ref.at[pl.ds(margin, nodes), :], enc_out, leave_sem.at[0])
    enc_leave.start()
    forward(1)

    def embed(start):
        embedded = jnp.dot(enc_ref[pl.ds(start, 128), :], w_in_full[...], preferred_element_type=F32)
        average = jnp.mean(embedded, axis=1, keepdims=True)
        centered = embedded - average
        spread = jnp.mean(centered * centered, axis=1, keepdims=True)
        normed_ref[pl.ds(start, 128), :] = (
            centered * lax.rsqrt(spread + 1e-05) * gain_ref[...]).astype(BF16)

    @pl.loop(0, nodes // 128, unroll=2)
    def _(i):
        embed(pl.multiple_of(margin + i * 128, 128))

    enc_up.wait_recv()
    enc_down.wait_recv()

    @pl.loop(0, margin // 128)
    def _(i):
        embed(pl.multiple_of(i * 128, 128))
        embed(pl.multiple_of(margin + nodes + i * 128, 128))

    forward(2)
    begin(groups)

    same_head = (lax.broadcasted_iota(jnp.int32, (gw, gw), 0) // head_size
                 == lax.broadcasted_iota(jnp.int32, (gw, gw), 1) // head_size).astype(BF16)
    contract_last = (((1,), (1,)), ((), ()))

    def unit_heads(block, scale):
        squares = block * block
        high = squares.astype(BF16)
        rest = (squares - high.astype(F32)).astype(BF16)
        total = (jnp.dot(high, same_head, preferred_element_type=F32)
                 + jnp.dot(rest, same_head, preferred_element_type=F32))
        return (block * lax.rsqrt(total * (1.0 / head_size) + 1e-06)).astype(BF16) * scale

    scale = jnp.asarray(head_size ** -0.5, BF16)
    one = jnp.asarray(1.0, BF16)

    def compute(g):
        for i in range(window // 512):
            span = pl.ds(i * 512, 512)
            part = jnp.dot(normed_ref[span, :], qkv_ref[g, :, pl.ds(gw, 2 * gw)],
                           preferred_element_type=F32)
            k_ref[span, :] = unit_heads(part[:, :gw], one)
            v_ref[span, :] = part[:, gw:].astype(BF16)
        part = jnp.dot(normed_ref[pl.ds(margin, nodes), :], qkv_ref[g, :, pl.ds(0, gw)],
                       preferred_element_type=F32)
        q_ref[...] = unit_heads(part, scale)

        @pl.loop(0, nodes // 128, unroll=2)
        def _(i):
            span = pl.ds(pl.multiple_of(i * 128, 128), 128)
            queries = q_ref[span, :]
            head_of = lax.broadcasted_iota(jnp.int32, (128, gw), 1) // head_size
            stacked = jnp.concatenate(
                [jnp.where(head_of == h, queries, jnp.zeros_like(queries))
                 for h in range(GROUP_HEADS)], axis=0)
            scores = lax.dot_general(stacked, k_ref[...], contract_last,
                                     preferred_element_type=F32)
            weights = jnp.exp(scores)
            total = jnp.sum(weights, axis=1, keepdims=True)
            out = jnp.dot(weights.astype(BF16), v_ref[...], preferred_element_type=F32)
            out = out * (1.0 / total)
            mixed = out[:128]
            for h in range(1, GROUP_HEADS):
                mixed = jnp.where(head_of == h, out[h * 128:(h + 1) * 128], mixed)
            att_ref[g, span, :] = mixed.astype(BF16)

    def leave(g):
        return pltpu.make_async_copy(
            att_ref.at[g], att_out.at[:, pl.ds(g * gw, gw)], leave_sem.at[2 + g])

    w_out_leave = pltpu.make_async_copy(out_ref, w_out_full, leave_sem.at[1])

    @pl.loop(0, groups)
    def _(g):
        for c in range(groups):
            @pl.when(g == c)
            def _():
                finish(c)
                if c == 0:
                    forward(groups - 1)
                if c == groups - 2:
                    forward(groups)
                if c:
                    leave(c - 1).start()
        compute(g)

    leave(groups - 1).start()
    finish(groups)
    w_out_leave.start()
    for g in range(groups):
        leave(g).wait()
    w_out_leave.wait()
    enc_leave.wait()
    for copy in (field_up, field_down, enc_up, enc_down):
        copy.wait_send()
    for c in range(groups + 1):
        drain(c)


def project(enc_ref, w_in_ref, att_ref, w_out_ref, latent_ref, update_ref):
    channels = w_in_ref.shape[0]
    latent_ref[...] = jnp.dot(enc_ref[:, :channels], w_in_ref[...],
                              preferred_element_type=F32).astype(BF16)
    update_ref[...] = jnp.dot(att_ref[...], w_out_ref[...],
                              preferred_element_type=F32).astype(BF16)


def shards(n, space, fields, cell_index, interp_weight, w_in, ln_gain, w_qkv, w_out):
    width = w_out.shape[1]
    blocks, per_block, _ = interp_weight.shape
    nodes = blocks * per_block
    channels, cells = fields.shape[1:]
    reach = cells // 4
    gw = width // HEADS * GROUP_HEADS
    groups = width // gw
    vmem = pl.BlockSpec(memory_space=pltpu.VMEM)
    hbm = pl.BlockSpec(memory_space=pl.ANY)
    dma = pltpu.SemaphoreType.DMA
    attended, w_out_full, encoded = pl.pallas_call(
        functools.partial(kernel, n, space),
        out_shape=[jax.ShapeDtypeStruct(shape, BF16)
                   for shape in ((nodes, width), (width, width), (nodes, 128))],
        in_specs=[pl.BlockSpec(memory_space=pltpu.SMEM), vmem, vmem, vmem, vmem, hbm, hbm],
        out_specs=[hbm, hbm, hbm],
        scratch_shapes=[
            pltpu.VMEM((channels, reach), BF16),
            pltpu.VMEM((channels, reach), BF16),
            pltpu.VMEM((cells + 2 * reach, 128), F32),
            pltpu.VMEM((blocks * 128, 128), F32),
            pltpu.VMEM((2 * nodes, 128), BF16),
            pltpu.VMEM((128, width), BF16),
            pltpu.VMEM((2 * nodes, width), BF16),
            pltpu.VMEM((groups, width, 3 * gw), BF16),
            pltpu.VMEM((width, width), BF16),
            pltpu.VMEM((nodes, gw), BF16),
            pltpu.VMEM((2 * nodes, gw), BF16),
            pltpu.VMEM((2 * nodes, gw), BF16),
            pltpu.VMEM((groups, nodes, gw), BF16),
            dma((3 * groups + 1,)), dma((groups + 2,)),
            dma((2,)), dma((2,)), dma((2,)), dma((2,)),
            dma((groups + 1, n - 1)), dma((groups + 1, n - 1)),
            dma((groups + 1, 2)), dma((groups + 1, 2)),
            dma((groups + 1, n - 1)), dma((groups + 1, n - 1)),
        ],
        compiler_params=pltpu.CompilerParams(
            collective_id=0, has_side_effects=True, vmem_limit_bytes=60 * 2**20),
    )(cell_index, fields[0], interp_weight, w_in, ln_gain[None], w_qkv, w_out)
    step = nodes // 2

    def by_row(size):
        return pl.BlockSpec((step, size), lambda i: (i, 0))

    def whole(array):
        return pl.BlockSpec(array.shape, lambda i: (0, 0))

    latent, update = pl.pallas_call(
        project,
        grid=(nodes // step,),
        out_shape=[jax.ShapeDtypeStruct((nodes, width), BF16)] * 2,
        in_specs=[by_row(128), whole(w_in), by_row(width), whole(w_out_full)],
        out_specs=[by_row(width), by_row(width)],
    )(encoded, w_in, attended, w_out_full)
    return latent[None], update[None]


def solution(mesh):
    placed = (
        P("dp", None, "space"),
        P("space", None),
        P("space", None, None),
        P(),
        P(),
        P("dp", None),
        P("dp", None),
    )
    return jax.shard_map(
        functools.partial(shards, mesh.shape["dp"], mesh.shape["space"]),
        mesh=mesh,
        in_specs=placed,
        out_specs=(P("dp", "space", None), P("dp", "space", None)),
        check_vma=False,
    )
```

profile of v0, /device:TPU:30, one launch (start us, length us, event | category | flops | bytes accessed | tf_op | source)
XLA Modules:
  0.0 133.2 jit_solution(3674348541730004668)
XLA Ops:
  0.6 128.2 %shard_map.86 = (bf16[512,1024]{1,0:T(8,128)(2,1)}, bf16[1024,1024]{1,0:T(8,128)(2,1)}, bf16[512,128]{1,0:T(8,128)(2,1)}) custom-call(s32[32,128]{1,0:T(8,128)} %index_ref.1, bf16[100,4096]{1,0:T(8,128)(2,1)} %bitcast.4, bf16[32,16,128]{2,1,0:T(8,128)(2,1)} %weight_ref.1, bf16[100,1024]{1,0:T(8,128)(2,1)} %w_in_ref.3, f32[1,1024]{1,0:T(1,128)} %bitcast.5, ...), custom_call_target="tpu_custom_call" | custom-call | tf_op jit(solution)/shard_map/pallas_call | solution.py:317
  128.8 4.4 %shard_map.87 = (bf16[512,1024]{1,0:T(8,128)(2,1)}, bf16[512,1024]{1,0:T(8,128)(2,1)}) custom-call(bf16[512,128]{1,0:T(8,128)(2,1)} %get-tuple-element.7.enc_ref, bf16[100,1024]{1,0:T(8,128)(2,1)} %w_in_ref.3, bf16[512,1024]{1,0:T(8,128)(2,1)} %get-tuple-element.8.att_ref, bf16[1024,1024]{1,0:T(8,128)(2,1)} %get-tuple-element.9.w_out_ref), custom_call_target="tpu_custom_call" | custom-call | tf_op jit(solution)/shard_map/pallas_call | solution.py:354
where the time goes:
time: 133 us
  Pallas kernels  133 us (100%)
    pallas_call x1, Pallas kernels, shards(): pl.pallas_call(functools.partial(kernel, n, space), out_shape=[jax.ShapeD...  128 us
    pallas_call x1, Pallas kernels, shards(): pl.pallas_call(project, grid=(nodes // step,), out_shape=[jax.ShapeDtypeS...  4.36 us

commit v1 on v0

v1 whole, which is shorter than its diff:
```python
import functools

import jax
import jax.numpy as jnp
from jax import lax
from jax.experimental import pallas as pl
from jax.experimental.pallas import tpu as pltpu
from jax.sharding import PartitionSpec as P

HEADS = 16
GROUP_HEADS = 4
F32, BF16 = jnp.float32, jnp.bfloat16
MESH = pl.DeviceIdType.MESH
OFFS = (0, -1, 1, 2)


def device_at(x, y, z, core):
    return lax.rem(y, 4) * 4 + x, z * 4 + (y // 4) * 2 + core


def kernel(
    index_hbm, field_hbm, weight_hbm, w_in_hbm, gain_hbm, w_qkv_hbm, w_out_hbm,
    att_out, w_out_full, enc_out,
    index_ref, field_ref, weight_ref, w_in_ref, gain_ref,
    low_ref, high_ref, cells_ref, picked_ref, enc_ref, w_in_full, normed_ref, qkv_ref, out_ref,
    q_ref, k_ref, v_ref, att_ref, stage_ref,
    load_sem, local_sem, leave_sem, field_send, field_recv, enc_send, enc_recv,
    nm_send, nm_recv, st_send, st_recv, sw_send, sw_recv, a_send, a_recv, ready_sem,
):
    d, s = lax.axis_index("dp"), lax.axis_index("space")
    x, y_low = lax.rem(d, 4), d // 4
    core, y_high, z = lax.rem(s, 2), lax.rem(s // 2, 2), s // 4
    y = y_high * 4 + y_low
    up, down = lax.rem(s + 1, 32), lax.rem(s + 31, 32)
    other = 1 - core
    partner = (d, s + 1 - 2 * core)
    far = (d, down + core * (up - down))
    wraps = (z == 0) & (y_high == 0) & (core == 0)
    wrapped = (z == 7) & (y_high == 1) & (core == 1)
    follows = ((core == 0) & jnp.logical_not(wraps)) | wrapped
    follow = follows.astype(jnp.int32)

    x_up, x_down = device_at(lax.rem(x + 1, 4), y, z, core), device_at(lax.rem(x + 3, 4), y, z, core)
    y_up, y_down = device_at(x, lax.rem(y + 1, 8), z, core), device_at(x, lax.rem(y + 7, 8), z, core)

    def either(first, second):
        return tuple(a + core * (b - a) for a, b in zip(first, second))

    p1, m1 = either(x_up, y_up), either(x_down, y_down)
    p2, m2 = either(y_up, x_up), either(y_down, x_down)
    stride1, stride2 = 1 + 3 * core, 4 - 3 * core
    place1, place2 = x + core * (y_low - x), y_low + core * (x - y_low)

    barrier = pltpu.get_barrier_semaphore()
    for peer in (p1, m1, p2, m2, partner):
        pl.semaphore_signal(barrier, inc=1, device_id=peer, device_id_type=MESH)

    @pl.when(jnp.logical_not(follows))
    def _():
        pl.semaphore_signal(barrier, inc=1, device_id=far, device_id_type=MESH)

    channels, cell_count = field_ref.shape
    reach = low_ref.shape[1]
    rows = w_qkv_hbm.shape[0]
    width = w_out_hbm.shape[1]
    groups, _, gw3 = qkv_ref.shape
    gw = gw3 // 3
    head_size = gw // GROUP_HEADS
    nodes = att_ref.shape[1]
    margin = nodes // 2
    window = nodes + 2 * margin
    blocks, per_block, slots = weight_ref.shape

    loads = [
        pltpu.make_async_copy(src, dst, load_sem.at[i])
        for i, (src, dst) in enumerate((
            (field_hbm, field_ref), (index_hbm, index_ref), (weight_hbm, weight_ref),
            (w_in_hbm, w_in_ref), (gain_hbm, gain_ref)))]
    local = []
    for g in range(groups):
        for t in range(3):
            local.append(pltpu.make_async_copy(
                w_qkv_hbm.at[:, pl.ds(pl.multiple_of(t * width + core * (width // 2) + g * gw, gw), gw)],
                qkv_ref.at[g, pl.ds(pl.multiple_of(d * rows, rows), rows), pl.ds(t * gw, gw)],
                local_sem.at[len(local)]))
    half = rows // 2
    local.append(pltpu.make_async_copy(
        w_out_hbm.at[pl.ds(pl.multiple_of(core * half, half), half), :], out_ref.at[d, core],
        local_sem.at[len(local)]))
    for copy in local[:3] + loads[:1] + local[3:] + loads[1:]:
        copy.start()

    pl.semaphore_wait(barrier, 5 + follow)

    @pl.when(follows)
    def _():
        pl.semaphore_signal(ready_sem, inc=1, device_id=far, device_id_type=MESH)

    def remote(src, dst, send, recv, device):
        return pltpu.make_async_remote_copy(
            src_ref=src, dst_ref=dst, send_sem=send, recv_sem=recv,
            device_id=device, device_id_type=MESH)

    field_up = remote(field_hbm.at[:, pl.ds(cell_count - reach, reach)], low_ref,
                      field_send.at[0], field_recv.at[0], (d, up))
    field_down = remote(field_hbm.at[:, pl.ds(0, reach)], high_ref,
                        field_send.at[1], field_recv.at[1], (d, down))

    def to_far():
        @pl.when(core == 0)
        def _():
            field_down.start()

        @pl.when(core == 1)
        def _():
            field_up.start()

    def far_when(role):
        @pl.when(role & jnp.logical_not(follows))
        def _():
            pl.semaphore_wait(ready_sem, 1)
            to_far()

    @pl.when(core == 0)
    def _():
        field_up.start()

    @pl.when(core == 1)
    def _():
        field_down.start()

    @pl.when(follows)
    def _():
        to_far()

    def slot(i, j):
        return lax.rem(place1 + i + 4, 4) * stride1 + lax.rem(place2 + j + 4, 4) * stride2

    def piece(c, at, side=None):
        if c < groups:
            lo, size = (0, rows) if side is None else (side * half, half)
            return qkv_ref.at[c, pl.ds(pl.multiple_of(at * rows + lo, size), size), :]
        lo, size = (0, half) if side is None else (side * (half // 2), half // 2)
        return out_ref.at[at, core, pl.ds(lo, size), :]

    def hop(c, i, ref, device):
        return remote(ref, ref, a_send.at[c, i], a_recv.at[c, i], device)

    def spread(c, j):
        ref = piece(c, slot(OFFS[j], 0))
        hop(c, 4 + 4 * j, ref, p2).start()
        hop(c, 5 + 4 * j, ref, m2).start()

    def begin(c):
        for copy in local[3 * c:3 * c + 3] if c < groups else local[-1:]:
            copy.wait()
        own = piece(c, slot(0, 0))
        hop(c, 0, own, p1).start()
        hop(c, 1, own, m1).start()
        spread(c, 0)

    def first(c):
        before, after = slot(-1, 0), slot(1, 0)
        hop(c, 0, piece(c, before), p1).wait_recv()
        hop(c, 2, piece(c, before, 0), p1).start()
        spread(c, 1)
        hop(c, 1, piece(c, after), p1).wait_recv()
        hop(c, 3, piece(c, after, 1), m1).start()
        spread(c, 2)

    def second(c):
        at = slot(2, 0)
        hop(c, 2, piece(c, at, 0), p1).wait_recv()
        hop(c, 3, piece(c, at, 1), p1).wait_recv()
        spread(c, 3)

    def across(c, j):
        before, after = slot(OFFS[j], -1), slot(OFFS[j], 1)
        hop(c, 4 + 4 * j, piece(c, before), p2).wait_recv()
        hop(c, 6 + 4 * j, piece(c, before, 0), p2).start()
        hop(c, 5 + 4 * j, piece(c, after), p2).wait_recv()
        hop(c, 7 + 4 * j, piece(c, after, 1), m2).start()

    def last(c):
        for j in range(4):
            at = slot(OFFS[j], 2)
            hop(c, 6 + 4 * j, piece(c, at, 0), p2).wait_recv()
            hop(c, 7 + 4 * j, piece(c, at, 1), p2).wait_recv()

    def drain(c):
        for i in range(20):
            ref = piece(c, slot(0, 0), 0 if i % 4 >= 2 else None)
            hop(c, i, ref, p1).wait_send()

    begin(0)
    begin(1)
    far_when(jnp.logical_not(wraps))

    unit = (lax.broadcasted_iota(jnp.int32, (channels, 128), 0)
            == lax.broadcasted_iota(jnp.int32, (channels, 128), 1)).astype(BF16)

    def turn(source, start, target):
        cells_ref[pl.ds(target, 512), :] = lax.dot_general(
            source[:, pl.ds(start, 512)], unit, (((0,), (0,)), ((), ())),
            preferred_element_type=F32)

    for copy in loads:
        copy.wait()

    @pl.loop(0, cell_count // 512, unroll=2)
    def _(i):
        turn(field_ref, pl.multiple_of(i * 512, 512), pl.multiple_of(reach + i * 512, 512))

    pad = w_in_full.shape[0]
    w_in_full[pl.ds(pad - 32, 32), :] = jnp.zeros((32, width), BF16)
    w_in_full[pl.ds(0, channels), :] = w_in_ref[...]

    first(0)
    across(0, 0)
    first(1)
    begin(groups)
    far_when(wraps)

    field_up.wait_recv()
    field_down.wait_recv()

    @pl.loop(0, reach // 512)
    def _(i):
        turn(low_ref, pl.multiple_of(i * 512, 512), pl.multiple_of(i * 512, 512))
        turn(high_ref, pl.multiple_of(i * 512, 512),
             pl.multiple_of(reach + cell_count + i * 512, 512))

    def gather(begin_at, end_at):
        @pl.loop(begin_at, end_at)
        def _(b):
            base = pl.multiple_of(b * slots, slots)
            for j in range(slots):
                picked_ref[pl.ds(base + j, 1), :] = cells_ref[pl.ds(index_ref[b, j], 1), :]

    across(1, 0)
    second(0)
    gather(0, blocks // 2)
    across(0, 1)
    across(0, 2)
    second(1)
    first(groups)
    gather(blocks // 2, blocks)
    across(0, 3)
    across(1, 1)
    across(1, 2)

    per_step = 8

    @pl.loop(0, blocks // per_step)
    def _(i):
        for j in range(per_step):
            b = i * per_step + j
            rows_b = picked_ref[pl.ds(pl.multiple_of(b * slots, slots), slots), :].astype(BF16)
            enc_ref[pl.ds(pl.multiple_of(b * per_block, per_block), per_block), :] = jnp.dot(
                weight_ref[b], rows_b, preferred_element_type=F32).astype(BF16)

    enc_far = remote(enc_ref.at[pl.ds(pl.multiple_of(core * margin, margin), margin), :],
                     enc_ref.at[pl.ds(nodes, margin), :], enc_send.at[0], enc_recv.at[0], far)
    enc_far.start()
    enc_leave = pltpu.make_async_copy(enc_ref.at[pl.ds(0, nodes), :], enc_out, leave_sem.at[0])
    enc_leave.start()

    def embed(start, target):
        embedded = jnp.dot(enc_ref[pl.ds(start, 128), :], w_in_full[...], preferred_element_type=F32)
        average = jnp.mean(embedded, axis=1, keepdims=True)
        centered = embedded - average
        spread_of = jnp.mean(centered * centered, axis=1, keepdims=True)
        normed_ref[pl.ds(target, 128), :] = (
            centered * lax.rsqrt(spread_of + 1e-05) * gain_ref[...]).astype(BF16)

    own = pl.multiple_of(margin + core * nodes, margin)
    theirs = pl.multiple_of(margin + other * nodes, margin)
    edge = pl.multiple_of(core * (window + nodes - margin), margin)
    their_edge = pl.multiple_of(other * (window + nodes - margin), margin)

    def share(i, start):
        ref = normed_ref.at[pl.ds(start, margin), :]
        return remote(ref, ref, nm_send.at[i], nm_recv.at[i], partner)

    for h in range(2):
        @pl.loop(0, 2, unroll=2)
        def _(i):
            embed(pl.multiple_of(h * margin + i * 128, 128), pl.multiple_of(own + h * margin + i * 128, 128))
        share(h, own + h * margin).start()
        if h == 0:
            across(1, 3)
            second(groups)
        else:
            across(groups, 0)

    same_head = (lax.broadcasted_iota(jnp.int32, (gw, gw), 0) // head_size
                 == lax.broadcasted_iota(jnp.int32, (gw, gw), 1) // head_size).astype(BF16)
    contract_last = (((1,), (1,)), ((), ()))

    def unit_heads(block, scale):
        squares = block * block
        high = squares.astype(BF16)
        rest = (squares - high.astype(F32)).astype(BF16)
        total = (jnp.dot(high, same_head, preferred_element_type=F32)
                 + jnp.dot(rest, same_head, preferred_element_type=F32))
        return (block * lax.rsqrt(total * (1.0 / head_size) + 1e-06)).astype(BF16) * scale

    scale = jnp.asarray(head_size ** -0.5, BF16)
    one = jnp.asarray(1.0, BF16)

    def keys_of(g, start, size):
        span = pl.ds(start, size)
        part = jnp.dot(normed_ref[span, :], qkv_ref[g, :, pl.ds(gw, 2 * gw)], preferred_element_type=F32)
        k_ref[g, span, :] = unit_heads(part[:, :gw], one)
        v_ref[g, span, :] = part[:, gw:].astype(BF16)

    def queries_of(g, start, size):
        part = jnp.dot(normed_ref[pl.ds(start, size), :], qkv_ref[g, :, pl.ds(0, gw)],
                       preferred_element_type=F32)
        q_ref[g, pl.ds(pl.multiple_of(start - margin, margin), size), :] = unit_heads(part, scale)

    last(0)
    last(1)

    @pl.loop(0, groups)
    def _(g):
        keys_of(g, own, nodes)
        queries_of(g, own, nodes)

    across(groups, 1)
    across(groups, 2)
    across(groups, 3)
    enc_far.wait_recv()

    @pl.loop(0, 2, unroll=2)
    def _(i):
        embed(pl.multiple_of(nodes + i * 128, 128), pl.multiple_of(edge + i * 128, 128))

    share(2, edge).start()
    share(0, theirs).wait_recv()
    share(1, theirs).wait_recv()

    @pl.loop(0, groups)
    def _(g):
        keys_of(g, theirs, nodes)
        queries_of(g, theirs, nodes)
        keys_of(g, edge, margin)

    last(groups)
    swap = remote(out_ref.at[:, core], out_ref.at[:, core], sw_send.at[0], sw_recv.at[0], partner)
    swap.start()
    share(2, their_edge).wait_recv()

    @pl.loop(0, groups)
    def _(g):
        keys_of(g, their_edge, margin)

    def attend(g, side, store):
        base = pl.multiple_of(side * nodes, nodes)

        @pl.loop(0, nodes // 128, unroll=2)
        def _(i):
            queries = q_ref[g, pl.ds(pl.multiple_of(base + i * 128, 128), 128), :]
            head_of = lax.broadcasted_iota(jnp.int32, (128, gw), 1) // head_size
            stacked = jnp.concatenate(
                [jnp.where(head_of == h, queries, jnp.zeros_like(queries))
                 for h in range(GROUP_HEADS)], axis=0)
            scores = lax.dot_general(stacked, k_ref[g, pl.ds(base, window), :], contract_last,
                                     preferred_element_type=F32)
            weights = jnp.exp(scores)
            total = jnp.sum(weights, axis=1, keepdims=True)
            out = jnp.dot(weights.astype(BF16), v_ref[g, pl.ds(base, window), :],
                          preferred_element_type=F32)
            out = out * (1.0 / total)
            mixed = out[:128]
            for h in range(1, GROUP_HEADS):
                mixed = jnp.where(head_of == h, out[h * 128:(h + 1) * 128], mixed)
            store(pl.ds(pl.multiple_of(i * 128, 128), 128), mixed.astype(BF16))

    def leave(i, j):
        return pltpu.make_async_copy(
            att_ref.at[j], att_out.at[:, pl.ds(pl.multiple_of(j * gw, gw), gw)], leave_sem.at[2 + i])

    def give(g):
        return remote(stage_ref.at[g], att_ref.at[core * groups + g], st_send.at[g], st_recv.at[g], partner)

    w_out_leave = pltpu.make_async_copy(out_ref, w_out_full, leave_sem.at[1])

    for g in range(groups):
        def to_stage(span, value):
            stage_ref[g, span, :] = value

        def to_own(span, value):
            att_ref[core * groups + g, span, :] = value

        attend(g, other, to_stage)
        give(g).start()
        attend(g, core, to_own)
        leave(g, core * groups + g).start()
        if g == 0:
            swap.wait_recv()
            w_out_leave.start()

    for g in range(groups):
        give(g).wait_recv()
        leave(groups + g, other * groups + g).start()
    for g in range(groups):
        leave(g, core * groups + g).wait()
        leave(groups + g, other * groups + g).wait()
    w_out_leave.wait()
    enc_leave.wait()
    for copy in (field_up, field_down, enc_far, swap):
        copy.wait_send()
    for i in range(3):
        share(i, own).wait_send()
    for g in range(groups):
        give(g).wait_send()
    for c in range(groups + 1):
        drain(c)


def project(enc_ref, w_in_ref, att_ref, w_out_ref, latent_ref, update_ref):
    channels = w_in_ref.shape[0]
    latent_ref[...] = jnp.dot(enc_ref[:, :channels], w_in_ref[...],
                              preferred_element_type=F32).astype(BF16)
    update_ref[...] = jnp.dot(att_ref[...], w_out_ref[...],
                              preferred_element_type=F32).astype(BF16)


def shards(n, fields, cell_index, interp_weight, w_in, ln_gain, w_qkv, w_out):
    width = w_out.shape[1]
    blocks, per_block, slots = interp_weight.shape
    nodes = blocks * per_block
    channels, cells = fields.shape[1:]
    reach = cells // 4
    gw = width // HEADS * GROUP_HEADS
    groups = width // gw // 2
    half = w_out.shape[0] // 2
    hbm = pl.BlockSpec(memory_space=pl.ANY)
    dma = pltpu.SemaphoreType.DMA
    attended, w_out_full, encoded = pl.pallas_call(
        kernel,
        out_shape=[jax.ShapeDtypeStruct(shape, BF16)
                   for shape in ((nodes, width), (n, 2, half, width), (nodes, 128))],
        in_specs=[hbm] * 7,
        out_specs=[hbm, hbm, hbm],
        scratch_shapes=[
            pltpu.SMEM((blocks, slots), jnp.int32),
            pltpu.VMEM((channels, cells), BF16),
            pltpu.VMEM((blocks, per_block, slots), BF16),
            pltpu.VMEM((channels, width), BF16),
            pltpu.VMEM((1, width), F32),
            pltpu.VMEM((channels, reach), BF16),
            pltpu.VMEM((channels, reach), BF16),
            pltpu.VMEM((cells + 2 * reach, 128), F32),
            pltpu.VMEM((blocks * 128, 128), F32),
            pltpu.VMEM((nodes + nodes // 2, 128), BF16),
            pltpu.VMEM((128, width), BF16),
            pltpu.VMEM((3 * nodes, width), BF16),
            pltpu.VMEM((groups, width, 3 * gw), BF16),
            pltpu.VMEM((n, 2, half, width), BF16),
            pltpu.VMEM((groups, 2 * nodes, gw), BF16),
            pltpu.VMEM((groups, 3 * nodes, gw), BF16),
            pltpu.VMEM((groups, 3 * nodes, gw), BF16),
            pltpu.VMEM((2 * groups, nodes, gw), BF16),
            pltpu.VMEM((groups, nodes, gw), BF16),
            dma((5,)), dma((3 * groups + 1,)), dma((2 * groups + 2,)),
            dma((2,)), dma((2,)), dma((1,)), dma((1,)),
            dma((3,)), dma((3,)), dma((groups,)), dma((groups,)), dma((1,)), dma((1,)),
            dma((groups + 1, 20)), dma((groups + 1, 20)),
            pltpu.SemaphoreType.REGULAR,
        ],
        compiler_params=pltpu.CompilerParams(
            collective_id=0, has_side_effects=True, vmem_limit_bytes=60 * 2**20),
    )(cell_index, fields[0], interp_weight, w_in, ln_gain[None], w_qkv, w_out)
    w_out_full = w_out_full.reshape(width, width)
    step = nodes // 2

    def by_row(size):
        return pl.BlockSpec((step, size), lambda i: (i, 0))

    def whole(array):
        return pl.BlockSpec(array.shape, lambda i: (0, 0))

    latent, update = pl.pallas_call(
        project,
        grid=(nodes // step,),
        out_shape=[jax.ShapeDtypeStruct((nodes, width), BF16)] * 2,
        in_specs=[by_row(128), whole(w_in), by_row(width), whole(w_out_full)],
        out_specs=[by_row(width), by_row(width)],
    )(encoded, w_in, attended, w_out_full)
    return latent[None], update[None]


def solution(mesh):
    placed = (
        P("dp", None, "space"),
        P("space", None),
        P("space", None, None),
        P(),
        P(),
        P("dp", None),
        P("dp", None),
    )
    return jax.shard_map(
        functools.partial(shards, mesh.shape["dp"]),
        mesh=mesh,
        in_specs=placed,
        out_specs=(P("dp", "space", None), P("dp", "space", None)),
        check_vma=False,
    )
```

time: 133 us -> 69.8 us (0.52)
  the two profiles are of different devices: /device:TPU:30 before, /device:TPU:1 now
where the time goes in v1:
time: 69.8 us; the launch traced here: 69.4 us
  Pallas kernels  68.8 us (99%)
    pallas_call x1, Pallas kernels, shards(): pl.pallas_call(kernel, out_shape=[jax.ShapeDtypeStruct(shape, BF16) for s...  64.4 us
    pallas_call x1, Pallas kernels, shards(): pl.pallas_call(project, grid=(nodes // step,), out_shape=[jax.ShapeDtypeS...  4.37 us

profile of v1, /device:TPU:1, one launch (start us, length us, event | category | flops | bytes accessed | tf_op | source)
XLA Modules:
  0.0 69.4 jit_solution(15873977233848977952)
XLA Ops:
  0.6 64.4 %shard_map.86 = (bf16[512,1024]{1,0:T(8,128)(2,1)}, bf16[16,2,32,1024]{3,2,1,0:T(8,128)(2,1)}, bf16[512,128]{1,0:T(8,128)(2,1)}) custom-call(s32[32,128]{1,0:T(8,128)} %index_hbm.1, bf16[100,4096]{1,0:T(8,128)(2,1)} %bitcast.6, bf16[32,16,128]{2,1,0:T(8,128)(2,1)} %weight_hbm.1, bf16[100,1024]{1,0:T(8,128)(2,1)} %w_in_ref.1, f32[1,1024]{1,0:T(1,128)} %bitcast.7, ...), custom_call_target="tpu_custom_call" | custom-call | tf_op jit(solution)/shard_map/pallas_call | solution.py:441
  65.0 4.4 %shard_map.87 = (bf16[512,1024]{1,0:T(8,128)(2,1)}, bf16[512,1024]{1,0:T(8,128)(2,1)}) custom-call(bf16[512,128]{1,0:T(8,128)(2,1)} %get-tuple-element.7.enc_ref, bf16[100,1024]{1,0:T(8,128)(2,1)} %w_in_ref.1, bf16[512,1024]{1,0:T(8,128)(2,1)} %get-tuple-element.8.att_ref, bf16[1024,1024]{1,0:T(8,128)(2,1)} %bitcast.5), custom_call_target="tpu_custom_call" | custom-call | tf_op jit(solution)/shard_map/pallas_call | solution.py:485

commit v2 on v1

v2 whole, which is shorter than its diff:
```python
import functools

import jax
import jax.numpy as jnp
from jax import lax
from jax.experimental import pallas as pl
from jax.experimental.pallas import tpu as pltpu
from jax.sharding import PartitionSpec as P

HEADS = 16
GROUP_HEADS = 4
F32, BF16 = jnp.float32, jnp.bfloat16
MESH = pl.DeviceIdType.MESH
OFFS = (0, -1, 1, 2)


def either(flag, first, second):
    return second if flag else first


def device_at(x, y, z, core):
    return lax.rem(y, 4) * 4 + x, z * 4 + (y // 4) * 2 + core


def kernel(
    index_hbm, field_hbm, weight_hbm, w_in_hbm, gain_hbm, w_qkv_hbm, w_out_hbm,
    att_out, out_ref, enc_out, w_in_out,
    index_ref, field_ref, weight_ref, w_in_ref, gain_ref,
    low_ref, high_ref, cells_ref, picked_ref, enc_ref, w_in_full, normed_ref, qkv_ref,
    q_ref, k_ref, v_ref, att_ref, stage_ref,
    load_sem, local_sem, leave_sem, field_send, field_recv, enc_send, enc_recv,
    nm_send, nm_recv, st_send, st_recv, sw_send, sw_recv, a_send, a_recv, ready_sem,
):
    d, s = lax.axis_index("dp"), lax.axis_index("space")
    x, y_low = lax.rem(d, 4), d // 4
    core, y_high, z = lax.rem(s, 2), lax.rem(s // 2, 2), s // 4
    y = y_high * 4 + y_low
    up, down = lax.rem(s + 1, 32), lax.rem(s + 31, 32)
    other = 1 - core
    partner = (d, s + 1 - 2 * core)
    far = (d, down + core * (up - down))
    wraps, wrapped = s == 0, s == 31

    along_x = [device_at(lax.rem(x + i, 4), y, z, core) for i in (1, 3, 2, 2)]
    along_y = [device_at(x, lax.rem(y + i, 8), z, core) for i in (1, 7, 2, 6)]
    near = along_x[:3] + along_y + [partner]

    barrier = pltpu.get_barrier_semaphore()
    for peer in near:
        pl.semaphore_signal(barrier, inc=1, device_id=peer, device_id_type=MESH)

    @pl.when(jnp.logical_not(wrapped))
    def _():
        pl.semaphore_signal(barrier, inc=1, device_id=far, device_id_type=MESH)

    channels, cell_count = field_ref.shape
    reach = low_ref.shape[1]
    rows = w_qkv_hbm.shape[0]
    width = w_out_hbm.shape[1]
    groups, _, gw3 = qkv_ref.shape
    gw = gw3 // 3
    head_size = gw // GROUP_HEADS
    nodes = att_ref.shape[1]
    margin = nodes // 2
    window = nodes + 2 * margin
    blocks, per_block, slots = weight_ref.shape

    loads = [
        pltpu.make_async_copy(src, dst, load_sem.at[i])
        for i, (src, dst) in enumerate((
            (field_hbm, field_ref), (index_hbm, index_ref), (weight_hbm, weight_ref),
            (w_in_hbm, w_in_ref), (gain_hbm, gain_ref)))]
    local = []
    for g in range(groups):
        for t in range(3):
            local.append(pltpu.make_async_copy(
                w_qkv_hbm.at[:, pl.ds(pl.multiple_of(t * width + core * (width // 2) + g * gw, gw), gw)],
                qkv_ref.at[g, pl.ds(pl.multiple_of(d * rows, rows), rows), pl.ds(t * gw, gw)],
                local_sem.at[len(local)]))
    half = rows // 2
    local.append(pltpu.make_async_copy(
        w_out_hbm.at[pl.ds(pl.multiple_of(core * half, half), half), :], out_ref.at[d, core],
        local_sem.at[len(local)]))
    for copy in local[:3] + loads[:1] + local[3:] + loads[1:]:
        copy.start()

    pl.semaphore_wait(barrier, len(near) + 1 - wraps.astype(jnp.int32))

    @pl.when(wrapped)
    def _():
        pl.semaphore_signal(ready_sem, inc=1, device_id=far, device_id_type=MESH)

    def remote(src, dst, send, recv, device):
        return pltpu.make_async_remote_copy(
            src_ref=src, dst_ref=dst, send_sem=send, recv_sem=recv,
            device_id=device, device_id_type=MESH)

    field_up = remote(field_hbm.at[:, pl.ds(cell_count - reach, reach)], low_ref,
                      field_send.at[0], field_recv.at[0], (d, up))
    field_down = remote(field_hbm.at[:, pl.ds(0, reach)], high_ref,
                        field_send.at[1], field_recv.at[1], (d, down))

    def to_far():
        @pl.when(core == 0)
        def _():
            field_down.start()

        @pl.when(core == 1)
        def _():
            field_up.start()

    @pl.when(core == 0)
    def _():
        field_up.start()

    @pl.when(core == 1)
    def _():
        field_down.start()

    turns = (1, 1, 0)

    def slot(c, i, j):
        place1, place2 = x + turns[c] * (y_low - x), y_low + turns[c] * (x - y_low)
        return (lax.rem(place1 + i + 4, 4) * (1 + 3 * turns[c])
                + lax.rem(place2 + j + 4, 4) * (4 - 3 * turns[c]))

    def piece(c, at, side=None):
        if c < groups:
            lo, size = (0, rows) if side is None else (side * half, half)
            return qkv_ref.at[c, pl.ds(pl.multiple_of(at * rows + lo, size), size), :]
        lo, size = (0, half) if side is None else (side * (half // 2), half // 2)
        return out_ref.at[at, core, pl.ds(lo, size), :]

    sides = (None, None, 0, 1)

    def hop(c, i, at, device):
        ref = piece(c, at, sides[i % 4])
        return remote(ref, ref, a_send.at[c, i], a_recv.at[c, i], device)

    def begin(c):
        for copy in local[3 * c:3 * c + 3] if c < groups else local[-1:]:
            copy.wait()
        for i in range(4):
            hop(c, i, slot(c, 0, 0), either(turns[c], along_x[i], along_y[i])).start()

    def spread(c, j):
        for i in range(2):
            hop(c, 4 + 4 * j + i, slot(c, OFFS[j], 0), either(turns[c], along_y[i], along_x[i])).start()

    def onward(c):
        hop(c, 0, slot(c, -1, 0), partner).wait_recv()
        spread(c, 1)
        hop(c, 1, slot(c, 1, 0), partner).wait_recv()
        spread(c, 2)
        hop(c, 2, slot(c, 2, 0), partner).wait_recv()
        hop(c, 3, slot(c, 2, 0), partner).wait_recv()
        spread(c, 3)

    def across(c, *js):
        for j in js:
            for i in range(2):
                at = slot(c, OFFS[j], 2 * i - 1)
                hop(c, 4 + 4 * j + i, at, partner).wait_recv()
                hop(c, 6 + 4 * j + i, at, either(turns[c], along_y[i], along_x[i])).start()

    def last(c):
        for j in range(4):
            for i in range(2):
                hop(c, 6 + 4 * j + i, slot(c, OFFS[j], 2), partner).wait_recv()

    def drain(c):
        for i in range(20):
            hop(c, i, slot(c, 0, 0), partner).wait_send()

    @pl.when(wrapped)
    def _():
        to_far()

    begin(0)

    @pl.when(jnp.logical_not(wraps | wrapped))
    def _():
        to_far()

    spread(0, 0)

    unit = (lax.broadcasted_iota(jnp.int32, (channels, 128), 0)
            == lax.broadcasted_iota(jnp.int32, (channels, 128), 1)).astype(BF16)

    def turn(source, start, target):
        cells_ref[pl.ds(target, 512), :] = lax.dot_general(
            source[:, pl.ds(start, 512)], unit, (((0,), (0,)), ((), ())),
            preferred_element_type=F32)

    for copy in loads:
        copy.wait()

    @pl.loop(0, cell_count // 512, unroll=2)
    def _(i):
        turn(field_ref, pl.multiple_of(i * 512, 512), pl.multiple_of(reach + i * 512, 512))

    pad = w_in_full.shape[0]
    w_in_full[pl.ds(pad - 32, 32), :] = jnp.zeros((32, width), BF16)
    w_in_full[pl.ds(0, channels), :] = w_in_ref[...]

    @pl.when(wraps)
    def _():
        pl.semaphore_wait(ready_sem, 1)
        to_far()

    w_in_leave = pltpu.make_async_copy(w_in_full, w_in_out, leave_sem.at[groups + 1])
    w_in_leave.start()
    onward(0)
    across(0, 0, 1)

    field_up.wait_recv()
    field_down.wait_recv()

    begin(1)
    spread(1, 0)

    @pl.when(jnp.logical_not(wrapped))
    def _():
        across(0, 2)

    @pl.loop(0, reach // 512)
    def _(i):
        turn(low_ref, pl.multiple_of(i * 512, 512), pl.multiple_of(i * 512, 512))
        turn(high_ref, pl.multiple_of(i * 512, 512),
             pl.multiple_of(reach + cell_count + i * 512, 512))

    def gather(begin_at, end_at):
        @pl.loop(begin_at, end_at)
        def _(b):
            base = pl.multiple_of(b * slots, slots)
            for j in range(slots):
                picked_ref[pl.ds(base + j, 1), :] = cells_ref[pl.ds(index_ref[b, j], 1), :]

    gather(0, blocks // 2)
    @pl.when(jnp.logical_not(wrapped))
    def _():
        across(0, 3)

    gather(blocks // 2, blocks)
    per_step = 8

    @pl.loop(0, blocks // per_step)
    def _(i):
        for j in range(per_step):
            b = i * per_step + j
            rows_b = picked_ref[pl.ds(pl.multiple_of(b * slots, slots), slots), :].astype(BF16)
            enc_ref[pl.ds(pl.multiple_of(b * per_block, per_block), per_block), :] = jnp.dot(
                weight_ref[b], rows_b, preferred_element_type=F32).astype(BF16)

    enc_far = remote(enc_ref.at[pl.ds(pl.multiple_of(core * margin, margin), margin), :],
                     enc_ref.at[pl.ds(nodes, margin), :], enc_send.at[0], enc_recv.at[0], far)
    enc_far.start()
    enc_leave = pltpu.make_async_copy(enc_ref.at[pl.ds(0, nodes), :], enc_out, leave_sem.at[0])
    enc_leave.start()

    def embed(start, target):
        embedded = jnp.dot(enc_ref[pl.ds(start, 128), :], w_in_full[...], preferred_element_type=F32)
        average = jnp.mean(embedded, axis=1, keepdims=True)
        centered = embedded - average
        spread_of = jnp.mean(centered * centered, axis=1, keepdims=True)
        normed_ref[pl.ds(target, 128), :] = (
            centered * lax.rsqrt(spread_of + 1e-05) * gain_ref[...]).astype(BF16)

    @pl.when(wrapped)
    def _():
        across(0, 2, 3)

    begin(groups)
    spread(groups, 0)
    own = pl.multiple_of(margin + core * nodes, margin)
    theirs = pl.multiple_of(margin + other * nodes, margin)
    edge = pl.multiple_of(core * (window + nodes - margin), margin)
    their_edge = pl.multiple_of(other * (window + nodes - margin), margin)

    def share(i, start):
        ref = normed_ref.at[pl.ds(start, margin), :]
        return remote(ref, ref, nm_send.at[i], nm_recv.at[i], partner)

    for h in range(2):
        @pl.loop(0, 2, unroll=2)
        def _(i):
            embed(pl.multiple_of(h * margin + i * 128, 128), pl.multiple_of(own + h * margin + i * 128, 128))
        share(h, own + h * margin).start()

    same_head = (lax.broadcasted_iota(jnp.int32, (gw, gw), 0) // head_size
                 == lax.broadcasted_iota(jnp.int32, (gw, gw), 1) // head_size).astype(BF16)

    def unit_heads(block, scale):
        squares = block * block
        total = jnp.dot(squares.astype(BF16), same_head, preferred_element_type=F32)
        return (block * lax.rsqrt(total * (1.0 / head_size) + 1e-06)).astype(BF16) * scale

    scale = jnp.asarray(head_size ** -0.5, BF16)
    one = jnp.asarray(1.0, BF16)

    def store_part(g, kind, start, size, part):
        span = pl.ds(start, size)
        if kind == 0:
            q_ref[g, pl.ds(pl.multiple_of(start - margin, margin), size), :] = unit_heads(part, scale)
        elif kind == 1:
            k_ref[g, :, span] = unit_heads(part, one).T
        else:
            v_ref[g, span, :] = part.astype(BF16)

    def rows_of(g, *pieces):
        held = None
        for kind, start, size in pieces:
            part = jnp.dot(normed_ref[pl.ds(start, size), :], qkv_ref[g, :, pl.ds(kind * gw, gw)],
                           preferred_element_type=F32)
            if held is not None:
                store_part(g, *held)
            held = (kind, start, size, part)
        store_part(g, *held)

    def all_of(start, size):
        return [(1, start, size), (0, start, size), (2, start, size)]

    def keys_at(start):
        return [(1, start, margin), (2, start, margin)]

    last(0)

    rows_of(0, *all_of(own, nodes))

    onward(1)
    share(0, theirs).wait_recv()
    share(1, theirs).wait_recv()

    rows_of(0, *all_of(theirs, nodes))
    across(1, 0, 1)
    enc_far.wait_recv()

    @pl.loop(0, 2, unroll=2)
    def _(i):
        embed(pl.multiple_of(nodes + i * 128, 128), pl.multiple_of(edge + i * 128, 128))

    share(2, edge).start()
    rows_of(0, *keys_at(edge))
    share(2, their_edge).wait_recv()
    rows_of(0, *keys_at(their_edge))

    swap = remote(out_ref.at[:, core], out_ref.at[:, core], sw_send.at[0], sw_recv.at[0], partner)

    def attend(g, side, store):
        base = pl.multiple_of(side * nodes, nodes)

        head_of = lax.broadcasted_iota(jnp.int32, (128, gw), 1) // head_size

        def scores_of(i):
            queries = q_ref[g, pl.ds(pl.multiple_of(base + i * 128, 128), 128), :]
            stacked = jnp.concatenate(
                [jnp.where(head_of == h, queries, jnp.zeros_like(queries))
                 for h in range(GROUP_HEADS)], axis=0)
            return jnp.dot(stacked, k_ref[g, :, pl.ds(base, window)], preferred_element_type=F32)

        steps = nodes // 128
        scores = scores_of(0)
        for i in range(steps):
            later = scores_of(i + 1) if i + 1 < steps else None
            weights = jnp.exp(scores)
            total = jnp.sum(weights, axis=1, keepdims=True)
            out = jnp.dot(weights.astype(BF16), v_ref[g, pl.ds(base, window), :],
                          preferred_element_type=F32)
            out = out * (1.0 / total)
            mixed = out[:128]
            for h in range(1, GROUP_HEADS):
                mixed = jnp.where(head_of == h, out[h * 128:(h + 1) * 128], mixed)
            store(pl.ds(i * 128, 128), mixed.astype(BF16))
            scores = later

    def columns(g):
        return att_out.at[:, pl.ds(pl.multiple_of((core * groups + g) * gw, gw), gw)]

    def leave(g):
        return pltpu.make_async_copy(att_ref.at[g], columns(g), leave_sem.at[1 + g])

    def give(g):
        return remote(stage_ref.at[g], columns(g), st_send.at[g], st_recv.at[g], partner)

    for g in range(groups):
        def to_stage(span, value):
            stage_ref[g, span, :] = value

        def to_own(span, value):
            att_ref[g, span, :] = value

        if g == 0:
            onward(groups)
            across(1, 2)
        attend(g, other, to_stage)
        give(g).start()
        if g == 0:
            across(1, 3)
            across(groups, 0)
        else:
            last(groups)
            swap.start()
        attend(g, core, to_own)
        leave(g).start()
        if g == 0:
            across(groups, 1, 2)
            last(1)

            @pl.loop(0, 2)
            def _(i):
                start = pl.multiple_of(margin + i * nodes, margin)
                rows_of(1, *keys_at(pl.multiple_of(i * (window + nodes - margin), margin)), *all_of(start, nodes))

            across(groups, 3)

    swap.wait_recv()
    for g in range(groups):
        give(g).wait_recv()
        leave(g).wait()
    enc_leave.wait()
    w_in_leave.wait()
    for copy in (field_up, field_down, enc_far, swap):
        copy.wait_send()
    for i in range(3):
        share(i, own).wait_send()
    for g in range(groups):
        give(g).wait_send()
    for c in range(groups + 1):
        drain(c)


def project(enc_ref, w_in_ref, att_ref, w_out_ref, latent_ref, update_ref):
    step = latent_ref.shape[0]
    span = pl.ds(pl.multiple_of(pl.program_id(0) * step, step), step)
    latent_ref[...] = jnp.dot(enc_ref[span, :], w_in_ref[...],
                              preferred_element_type=F32).astype(BF16)
    update_ref[...] = jnp.dot(att_ref[span, :], w_out_ref[...],
                              preferred_element_type=F32).astype(BF16)


def shards(n, fields, cell_index, interp_weight, w_in, ln_gain, w_qkv, w_out):
    width = w_out.shape[1]
    blocks, per_block, slots = interp_weight.shape
    nodes = blocks * per_block
    channels, cells = fields.shape[1:]
    reach = cells // 4
    gw = width // HEADS * GROUP_HEADS
    groups = width // gw // 2
    half = w_out.shape[0] // 2
    hbm = pl.BlockSpec(memory_space=pl.ANY)
    free = pl.BlockSpec(memory_space=pl.ANY)
    dma = pltpu.SemaphoreType.DMA
    attended, w_out_full, encoded, w_in_full = pl.pallas_call(
        kernel,
        out_shape=[jax.ShapeDtypeStruct(shape, BF16)
                   for shape in ((nodes, width), (n, 2, half, width), (nodes, 128), (128, width))],
        in_specs=[hbm] * 7,
        out_specs=[free] * 4,
        scratch_shapes=[
            pltpu.SMEM((blocks, slots), jnp.int32),
            pltpu.VMEM((channels, cells), BF16),
            pltpu.VMEM((blocks, per_block, slots), BF16),
            pltpu.VMEM((channels, width), BF16),
            pltpu.VMEM((1, width), F32),
            pltpu.VMEM((channels, reach), BF16),
            pltpu.VMEM((channels, reach), BF16),
            pltpu.VMEM((cells + 2 * reach, 128), F32),
            pltpu.VMEM((blocks * 128, 128), F32),
            pltpu.VMEM((nodes + nodes // 2, 128), BF16),
            pltpu.VMEM((128, width), BF16),
            pltpu.VMEM((3 * nodes, width), BF16),
            pltpu.VMEM((groups, width, 3 * gw), BF16),
            pltpu.VMEM((groups, 2 * nodes, gw), BF16),
            pltpu.VMEM((groups, gw, 3 * nodes), BF16),
            pltpu.VMEM((groups, 3 * nodes, gw), BF16),
            pltpu.VMEM((groups, nodes, gw), BF16),
            pltpu.VMEM((groups, nodes, gw), BF16),
            dma((5,)), dma((3 * groups + 1,)), dma((groups + 2,)),
            dma((2,)), dma((2,)), dma((1,)), dma((1,)),
            dma((3,)), dma((3,)), dma((groups,)), dma((groups,)), dma((1,)), dma((1,)),
            dma((groups + 1, 20)), dma((groups + 1, 20)),
            pltpu.SemaphoreType.REGULAR,
        ],
        compiler_params=pltpu.CompilerParams(
            collective_id=0, has_side_effects=True, vmem_limit_bytes=28 * 2**20),
    )(*(pltpu.with_memory_space_constraint(a, pltpu.HBM) for a in (
        cell_index, fields[0], interp_weight, w_in, ln_gain[None], w_qkv, w_out)))
    w_out_full = w_out_full.reshape(width, width)
    step = nodes // 4

    def by_row(size):
        return pl.BlockSpec((step, size), lambda i: (i, 0))

    vmem = pl.BlockSpec(memory_space=pltpu.VMEM)
    latent, update = pl.pallas_call(
        project,
        grid=(nodes // step,),
        out_shape=[jax.ShapeDtypeStruct((nodes, width), BF16)] * 2,
        in_specs=[vmem] * 4,
        out_specs=[by_row(width), by_row(width)],
        compiler_params=pltpu.CompilerParams(vmem_limit_bytes=24 * 2**20),
    )(encoded, w_in_full, attended, w_out_full)
    return latent[None], update[None]


def solution(mesh):
    placed = (
        P("dp", None, "space"),
        P("space", None),
        P("space", None, None),
        P(),
        P(),
        P("dp", None),
        P("dp", None),
    )
    return jax.shard_map(
        functools.partial(shards, mesh.shape["dp"]),
        mesh=mesh,
        in_specs=placed,
        out_specs=(P("dp", "space", None), P("dp", "space", None)),
        check_vma=False,
    )
```

time: 69.8 us -> 64.3 us (0.921)
  Pallas kernels: 68.8 us -> 63.5 us
    pallas_call x1, Pallas kernels: 64.4 us -> 60.6 us  [shards(): pl.pallas_call(kernel, out_shape=[jax.ShapeDtypeStruct(shape, BF16) for s...]
    pallas_call x1, Pallas kernels: 4.37 us -> 2.94 us  [shards(): pl.pallas_call(project, grid=(nodes // step,), out_shape=[jax.ShapeDtypeS...]
where the time goes in v2:
time: 64.3 us; the launch traced here: 64.2 us
  Pallas kernels  63.5 us (99%)
    pallas_call x1, Pallas kernels, shards(): pl.pallas_call(kernel, out_shape=[jax.ShapeDtypeStruct(shape, BF16) for s...  60.6 us
    pallas_call x1, Pallas kernels, shards(): pl.pallas_call(project, grid=(nodes // step,), out_shape=[jax.ShapeDtypeS...  2.94 us

profile of v2, /device:TPU:1, one launch (start us, length us, event | category | flops | bytes accessed | tf_op | source)
XLA Modules:
  0.0 64.2 jit_solution(16713795317288052961)
XLA Ops:
  0.6 60.6 %shard_map.86 = (bf16[512,1024]{1,0:T(8,128)(2,1)S(1)}, bf16[16,2,32,1024]{3,2,1,0:T(8,128)(2,1)S(1)}, bf16[512,128]{1,0:T(8,128)(2,1)S(1)}, bf16[128,1024]{1,0:T(8,128)(2,1)S(1)}) custom-call(s32[32,128]{1,0:T(8,128)} %index_hbm.1, bf16[100,4096]{1,0:T(8,128)(2,1)} %bitcast.6, bf16[32,16,128]{2,1,0:T(8,128)(2,1)} %weight_hbm.1, bf16[100,1024]{1,0:T(8,128)(2,1)} %w_in_hbm.1, ...), custom_call_target="tpu_custom_call" | custom-call | tf_op jit(solution)/shard_map/pallas_call | solution.py:453
  61.2 2.9 %shard_map.87 = (bf16[512,1024]{1,0:T(8,128)(2,1)}, bf16[512,1024]{1,0:T(8,128)(2,1)}) custom-call(bf16[512,128]{1,0:T(8,128)(2,1)S(1)} %get-tuple-element.8.enc_ref, bf16[128,1024]{1,0:T(8,128)(2,1)S(1)} %get-tuple-element.9.w_in_ref, bf16[512,1024]{1,0:T(8,128)(2,1)S(1)} %get-tuple-element.10.att_ref, bf16[1024,1024]{1,0:T(8,128)(2,1)S(1)} %bitcast.5), custom_call_target="tpu_custom_call" | custom-call | tf_op jit(solution)/shard_map/pallas_call | solution.py:495

commit v3 on v2

--- a/solution.py
+++ b/solution.py
@@ -27,7 +27,7 @@
     att_out, out_ref, enc_out, w_in_out,
     index_ref, field_ref, weight_ref, w_in_ref, gain_ref,
     low_ref, high_ref, cells_ref, picked_ref, enc_ref, w_in_full, normed_ref, qkv_ref,
-    q_ref, k_ref, v_ref, att_ref, stage_ref,
+    q_ref, k_ref, v_ref, result_ref,
     load_sem, local_sem, leave_sem, field_send, field_recv, enc_send, enc_recv,
     nm_send, nm_recv, st_send, st_recv, sw_send, sw_recv, a_send, a_recv, ready_sem,
 ):
@@ -60,7 +60,7 @@
     groups, _, gw3 = qkv_ref.shape
     gw = gw3 // 3
     head_size = gw // GROUP_HEADS
-    nodes = att_ref.shape[1]
+    nodes = result_ref.shape[2]
     margin = nodes // 2
     window = nodes + 2 * margin
     blocks, per_block, slots = weight_ref.shape
@@ -211,13 +211,17 @@
     w_in_leave = pltpu.make_async_copy(w_in_full, w_in_out, leave_sem.at[groups + 1])
     w_in_leave.start()
     onward(0)
+    def begin_next():
+        begin(1)
+        spread(1, 0)
+
+    pl.when(s < 4)(begin_next)
     across(0, 0, 1)
 
     field_up.wait_recv()
     field_down.wait_recv()
 
-    begin(1)
-    spread(1, 0)
+    pl.when(s >= 4)(begin_next)
 
     @pl.when(jnp.logical_not(wrapped))
     def _():
@@ -332,17 +336,32 @@
     share(1, theirs).wait_recv()
 
     rows_of(0, *all_of(theirs, nodes))
-    across(1, 0, 1)
-    enc_far.wait_recv()
-
-    @pl.loop(0, 2, unroll=2)
-    def _(i):
-        embed(pl.multiple_of(nodes + i * 128, 128), pl.multiple_of(edge + i * 128, 128))
-
-    share(2, edge).start()
-    rows_of(0, *keys_at(edge))
-    share(2, their_edge).wait_recv()
-    rows_of(0, *keys_at(their_edge))
+    across(1, 0)
+
+    @pl.when(s < 2)
+    def _():
+        across(1, 1)
+
+    def own_edge():
+        enc_far.wait_recv()
+
+        @pl.loop(0, 2, unroll=2)
+        def _(i):
+            embed(pl.multiple_of(nodes + i * 128, 128), pl.multiple_of(edge + i * 128, 128))
+
+        share(2, edge).start()
+        rows_of(0, *keys_at(edge))
+
+    def other_edge():
+        share(2, their_edge).wait_recv()
+        rows_of(0, *keys_at(their_edge))
+
+    pl.when(s != 0)(own_edge)
+    @pl.when(s >= 2)
+    def _():
+        across(1, 1)
+
+    pl.when(s != 1)(other_edge)
 
     swap = remote(out_ref.at[:, core], out_ref.at[:, core], sw_send.at[0], sw_recv.at[0], partner)
 
@@ -377,41 +396,44 @@
         return att_out.at[:, pl.ds(pl.multiple_of((core * groups + g) * gw, gw), gw)]
 
     def leave(g):
-        return pltpu.make_async_copy(att_ref.at[g], columns(g), leave_sem.at[1 + g])
+        return pltpu.make_async_copy(result_ref.at[1, g], columns(g), leave_sem.at[1 + g])
 
     def give(g):
-        return remote(stage_ref.at[g], columns(g), st_send.at[g], st_recv.at[g], partner)
-
+        return remote(result_ref.at[0, g], columns(g), st_send.at[g], st_recv.at[g], partner)
+
+    swapped = (s == 1).astype(jnp.int32)
     for g in range(groups):
-        def to_stage(span, value):
-            stage_ref[g, span, :] = value
-
-        def to_own(span, value):
-            att_ref[g, span, :] = value
+        earlier = swapped if g == 0 else 0
+
+        def to_place(place):
+            def store(span, value):
+                result_ref[place, g, span, :] = value
+            return store
 
         if g == 0:
             onward(groups)
             across(1, 2)
-        attend(g, other, to_stage)
-        give(g).start()
+        attend(g, other + earlier * (core - other), to_place(earlier))
         if g == 0:
             across(1, 3)
             across(groups, 0)
+            pl.when(s == 0)(own_edge)
+            pl.when(s == 1)(other_edge)
         else:
             last(groups)
             swap.start()
-        attend(g, core, to_own)
+            give(g).start()
+        attend(g, core + earlier * (other - core), to_place(1 - earlier))
         leave(g).start()
         if g == 0:
-            across(groups, 1, 2)
+            give(g).start()
+            across(groups, 1, 2, 3)
             last(1)
 
             @pl.loop(0, 2)
             def _(i):
                 start = pl.multiple_of(margin + i * nodes, margin)
                 rows_of(1, *keys_at(pl.multiple_of(i * (window + nodes - margin), margin)), *all_of(start, nodes))
-
-            across(groups, 3)
 
     swap.wait_recv()
     for g in range(groups):
@@ -473,8 +495,7 @@
             pltpu.VMEM((groups, 2 * nodes, gw), BF16),
             pltpu.VMEM((groups, gw, 3 * nodes), BF16),
             pltpu.VMEM((groups, 3 * nodes, gw), BF16),
-            pltpu.VMEM((groups, nodes, gw), BF16),
-            pltpu.VMEM((groups, nodes, gw), BF16),
+            pltpu.VMEM((2, groups, nodes, gw), BF16),
             dma((5,)), dma((3 * groups + 1,)), dma((groups + 2,)),
             dma((2,)), dma((2,)), dma((1,)), dma((1,)),
             dma((3,)), dma((3,)), dma((groups,)), dma((groups,)), dma((1,)), dma((1,)),

time: 64.3 us -> 63.1 us (0.981)
  Pallas kernels: 63.5 us -> 61.9 us
    pallas_call x1, Pallas kernels: 60.6 us -> 58.9 us  [shards(): pl.pallas_call(kernel, out_shape=[jax.ShapeDtypeStruct(shape, BF16) for s...]
where the time goes in v3:
time: 63.1 us; the launch traced here: 62.5 us
  Pallas kernels  61.9 us (98%)
  between operations  0.64 us (1%)
    pallas_call x1, Pallas kernels, shards(): pl.pallas_call(kernel, out_shape=[jax.ShapeDtypeStruct(shape, BF16) for s...  58.9 us
    pallas_call x1, Pallas kernels, shards(): pl.pallas_call(project, grid=(nodes // step,), out_shape=[jax.ShapeDtypeS...  2.94 us

profile of v3, /device:TPU:1, one launch (start us, length us, event | category | flops | bytes accessed | tf_op | source)
XLA Modules:
  0.0 62.5 jit_solution(7154558353532664340)
XLA Ops:
  0.6 58.9 %shard_map.86 = (bf16[512,1024]{1,0:T(8,128)(2,1)S(1)}, bf16[16,2,32,1024]{3,2,1,0:T(8,128)(2,1)S(1)}, bf16[512,128]{1,0:T(8,128)(2,1)S(1)}, bf16[128,1024]{1,0:T(8,128)(2,1)S(1)}) custom-call(s32[32,128]{1,0:T(8,128)} %index_hbm.1, bf16[100,4096]{1,0:T(8,128)(2,1)} %bitcast.6, bf16[32,16,128]{2,1,0:T(8,128)(2,1)} %weight_hbm.1, bf16[100,1024]{1,0:T(8,128)(2,1)} %w_in_hbm.1, ...), custom_call_target="tpu_custom_call" | custom-call | tf_op jit(solution)/shard_map/pallas_call | solution.py:475
  59.6 2.9 %shard_map.87 = (bf16[512,1024]{1,0:T(8,128)(2,1)}, bf16[512,1024]{1,0:T(8,128)(2,1)}) custom-call(bf16[512,128]{1,0:T(8,128)(2,1)S(1)} %get-tuple-element.8.enc_ref, bf16[128,1024]{1,0:T(8,128)(2,1)S(1)} %get-tuple-element.9.w_in_ref, bf16[512,1024]{1,0:T(8,128)(2,1)S(1)} %get-tuple-element.10.att_ref, bf16[1024,1024]{1,0:T(8,128)(2,1)S(1)} %bitcast.5), custom_call_target="tpu_custom_call" | custom-call | tf_op jit(solution)/shard_map/pallas_call | solution.py:516
